TPU v7x, 512 devices: a whole 4x4x16 slice. The times are simulated.
512 devices in a mesh: tm: 128 (over x, z, core), space: 4 (over y).
Axes of the slice: x: 4, y: 4, z: 16, core: 2. Of those that a mesh axis runs over, the one named last changes fastest.
Arguments:
- forcing: bfloat16 [2048, 256, 256], P('tm', 'space'), may hold values from -0.59765625 to 0.59765625
- starting_heat: bfloat16 [256, 256], P('space'), may hold values from -3 to 3, as said below
Outputs:
- heat_history: float32 [2048, 256, 256], P('tm', 'space')
- history: float32 [2, 512], P(None, 'tm')
- change: float32 [2, 512], P(None, 'tm')
Inputs may be any that keep to these rules, and one draw needn't show every extreme that they name: starting_heat is a combination of the 64 sine modes with both indices from 1 to 8, scaled so that its largest magnitude is 3.
All inputs are finite; a program needn't handle non-finite values.
Results may differ from a plain program's by a relative error of at most 0.0016.
Values may be sent and summed in bfloat16 or wider, within the bound.
A program may use at most 64 MiB of HBM per device.

v0:
```python
import math

import jax
import jax.numpy as jnp
from jax import lax
from jax.sharding import Mesh
from jax.sharding import PartitionSpec as P

FINE_FACTOR = 4
COARSE_FACTOR = 4
ITERS = 2
TM = ("tm_0", "tm_1", "tm_2")


DURATION = 0.004


def passed_along(block, axis, distance):
    devices = range(lax.axis_size(axis))
    route = [(i - distance, i) for i in devices if i - distance in devices]
    return lax.ppermute(block, axis, route)


def nothing_yet(array, identity):
    return jax.tree.map(
        lambda a, e: jnp.broadcast_to(jnp.asarray(e, a.dtype), a.shape), array, identity
    )


def carried_in(array, axes, combine, identity, reverse):
    before = start = nothing_yet(array, identity)
    running = array
    for axis in reversed(axes):
        devices, mine = lax.axis_size(axis), lax.axis_index(axis)
        pieces = jax.tree.map(lambda part: lax.all_gather(part, axis), running)
        inside, running = start, start
        for k in reversed(range(devices)) if reverse else range(devices):
            passed = k > mine if reverse else k < mine
            running = combine(running, jax.tree.map(lambda part: part[k], pieces))
            inside = jax.tree.map(lambda new, old: jnp.where(passed, new, old), running, inside)
        before = combine(inside, before)
    return before


def sine_table(sample_locations, number_type):
    numbers = jnp.arange(1, sample_locations + 1, dtype=jnp.int32)
    product = numbers[:, None] * numbers[None, :] % (2 * (sample_locations + 1))
    angles = jnp.pi * product.astype(jnp.float32) / (sample_locations + 1)
    return (math.sqrt(2.0 / (sample_locations + 1)) * jnp.sin(angles)).astype(number_type)


def eigenvalues(sample_locations, first_mode, mode_count):
    numbers = (first_mode + jnp.arange(mode_count, dtype=jnp.int32) + 1).astype(jnp.float32)
    halves = jnp.sin(jnp.pi * numbers / (2 * (sample_locations + 1)))
    return 4.0 * (sample_locations + 1) ** 2 * halves * halves


def smoothing_pass(starts, sources, factor):
    current = starts
    visited = []
    for column in range(sources.shape[1] - 1):
        current = factor * current + sources[:, column]
        visited.append(current)
    return visited


def compose_powers(earlier, later):
    return (earlier[0] * later[0], later[0] * earlier[1] + later[1])


def per_device(forcing, starting_heat):
    step_count, row_count, sample_locations = forcing.shape
    block_width = sample_locations // lax.axis_size("space")
    intervals = step_count // FINE_FACTOR
    blocks = intervals // COARSE_FACTOR
    steps_all = step_count * lax.axis_size(TM)
    table_half = sine_table(sample_locations, jnp.bfloat16)
    table_full = sine_table(sample_locations, jnp.float32)
    stacked = jnp.concatenate([starting_heat[None], forcing], axis=0)
    halved = jnp.dot(
        stacked.reshape(-1, sample_locations), table_half, preferred_element_type=jnp.float32
    )
    halved = halved.astype(jnp.bfloat16).reshape(step_count + 1, row_count, sample_locations)
    turned = lax.all_to_all(halved, "space", split_axis=2, concat_axis=1, tiled=True)
    spectra = jnp.einsum("xi,tiy->txy", table_half, turned, preferred_element_type=jnp.float32)
    first_mode = lax.axis_index("space") * block_width
    decay_rates = (
        eigenvalues(sample_locations, 0, sample_locations)[:, None]
        + eigenvalues(sample_locations, first_mode, block_width)[None, :]
    )
    increment_duration = DURATION / steps_all
    per_increment_factor = 1.0 / (1.0 + increment_duration * decay_rates)
    mid_gain = 1.0 / (1.0 + FINE_FACTOR * increment_duration * decay_rates)
    top_gain = 1.0 / (1.0 + FINE_FACTOR * COARSE_FACTOR * increment_duration * decay_rates)
    block_gain = top_gain
    for block_index in range(1, blocks):
        block_gain = block_gain * top_gain
    start_field = spectra[0]
    sources = (per_increment_factor * spectra[1:]).reshape(
        intervals, FINE_FACTOR, sample_locations, block_width
    )
    at_start = lax.axis_index(TM) == 0
    values = jnp.zeros((intervals, sample_locations, block_width), jnp.float32)
    pinned_boundary = jnp.where(at_start, start_field, jnp.zeros_like(start_field))
    norm_rows = []
    corr_rows = []
    value_rows = []
    for iteration in range(ITERS):
        ends_rest = smoothing_pass(values[:-1], sources[1:], per_increment_factor)[-1]
        relaxed_rest = per_increment_factor * ends_rest + sources[1:, -1]
        arrived = passed_along(relaxed_rest[-1], TM, 1)
        ends_first = smoothing_pass(pinned_boundary[None], sources[:1], per_increment_factor)[-1]
        relaxed = jnp.concatenate(
            [per_increment_factor * ends_first + sources[:1, -1], relaxed_rest], 0
        )
        arrived = jnp.where(at_start, start_field, arrived)
        ends_two = smoothing_pass(
            jnp.concatenate([arrived[None], relaxed[:-1]], 0), sources, per_increment_factor
        )[-1]
        residual = sources[:, -1] + per_increment_factor * ends_two - relaxed
        local_norms = jnp.sum(residual * residual, axis=(1, 2))
        coarse_rhs = residual.reshape(blocks, COARSE_FACTOR, sample_locations, block_width)
        running = coarse_rhs[:, 0]
        for column in range(1, COARSE_FACTOR):
            running = mid_gain * running + coarse_rhs[:, column]
        local_end = running[0]
        for block_index in range(1, blocks):
            local_end = top_gain * local_end + running[block_index]
        prefix = carried_in(
            (block_gain, local_end),
            TM,
            compose_powers,
            (jnp.ones_like(block_gain), jnp.zeros_like(local_end)),
            False,
        )
        incoming_value = prefix[1]
        coarse_list = []
        current = incoming_value
        for block_index in range(blocks):
            current = top_gain * current + running[block_index]
            coarse_list.append(current)
        coarse_values = jnp.stack(coarse_list)
        begins = jnp.concatenate([incoming_value[None], coarse_values[:-1]], 0)
        pieces = smoothing_pass(begins, coarse_rhs, mid_gain)
        correction = jnp.stack(pieces + [coarse_values], axis=1).reshape(
            intervals, sample_locations, block_width
        )
        values = relaxed + correction
        corr_sq = jnp.sum(correction * correction, axis=(1, 2))
        value_sq = jnp.sum(values * values, axis=(1, 2))
        norm_rows.append(local_norms)
        corr_rows.append(corr_sq)
        value_rows.append(value_sq)
        pinned_boundary = arrived + incoming_value
    starts = jnp.concatenate([pinned_boundary[None], values[:-1]], 0)
    inside = smoothing_pass(starts, sources, per_increment_factor)
    spectral_path = jnp.stack(inside + [values], axis=1).reshape(
        step_count, sample_locations, block_width
    )
    rows_back = jnp.einsum(
        "xi,tiy->txy", table_full, spectral_path, precision=lax.Precision.HIGHEST
    ).astype(jnp.bfloat16)
    returned = lax.all_to_all(rows_back, "space", split_axis=1, concat_axis=2, tiled=True)
    physical_rows = jnp.dot(
        returned.reshape(-1, sample_locations), table_half, preferred_element_type=jnp.float32
    )
    heat_history = physical_rows.reshape(step_count, row_count, sample_locations)
    norm_total, corr_total, value_total = lax.psum(
        (jnp.stack(norm_rows), jnp.stack(corr_rows), jnp.stack(value_rows)), "space"
    )
    history = jnp.sqrt(norm_total / (sample_locations * sample_locations))
    change = jnp.sqrt(corr_total / value_total)
    return (heat_history, history, change)


def solution(mesh):
    torus = Mesh(
        mesh.devices.reshape(4, 16, 2, mesh.shape["space"]), ("tm_0", "tm_1", "tm_2", "space")
    )
    in_specs = (P(TM, "space", None), P("space", None))
    out_specs = (P(TM, "space", None), P(None, TM), P(None, TM))
    return jax.shard_map(
        per_device, mesh=torus, in_specs=in_specs, out_specs=out_specs, check_vma=False
    )
```

profile of v0, /device:TPU:2, one launch (start us, length us, event | category | flops | bytes accessed | tf_op | source)
XLA Modules:
  0.0 344.0 jit_solution(6971806661333122464)
XLA Ops:
  10.6 1.6 reshape.2401
  12.2 4.5 %all-to-all-start = ((bf16[4,2,34816]{2,1,0:T(2,128)(2,1)}), bf16[4,2,34816]{2,1,0:T(2,128)(2,1)S(1)}, u32[]{:S(2)}, u32[]{:S(2)}) async-start(bf16[4,2,34816]{2,1,0:T(2,128)(2,1)} %reshape.2401), calls=%async_computation | async-start | bytes 1114112 | tf_op jit(solution)/shard_map/all_to_all | solution.py:84
  16.9 9.7 %all-to-all-done = bf16[4,2,34816]{2,1,0:T(2,128)(2,1)S(1)} async-done(((bf16[4,2,34816]{2,1,0:T(2,128)(2,1)}), bf16[4,2,34816]{2,1,0:T(2,128)(2,1)S(1)}, u32[]{:S(2)}, u32[]{:S(2)}) %all-to-all-start) | async-done | bytes 557088 | tf_op jit(solution)/shard_map/all_to_all | solution.py:84
  27.8 1.9 copy.55
  29.7 2.1 all_to_all.27
  33.5 1.9 collective-permute-start
  35.6 9.5 %collective-permute-done = f32[256,64]{0,1:T(8,128)S(1)} collective-permute-done((f32[256,64]{0,1:T(8,128)S(1)}, f32[256,64]{0,1:T(8,128)S(1)}, u32[]{:S(2)}, u32[]{:S(2)}) %collective-permute-start) | collective-permute-done | bytes 65568 | tf_op jit(solution)/shard_map/ppermute | solution.py:21
  45.7 1.9 all_gather.18
  47.6 1.9 all_gather.21
  51.1 67.7 %all-gather.4.cloned.1.call-done = f32[16,256,64]{1,2,0:T(8,128)} async-done(((f32[1,256,64]{1,2,0:T(8,128)}), f32[16,256,64]{1,2,0:T(8,128)}) %all-gather.4.cloned.1.call-update) | async-done | bytes 1048592 | tf_op jit(solution)/shard_map/all_gather | solution.py:35
  118.7 69.9 %all-gather.6.cloned.1.call-done = f32[16,256,64]{1,2,0:T(8,128)} async-done(((f32[1,256,64]{1,2,0:T(8,128)}), f32[16,256,64]{1,2,0:T(8,128)}) %all-gather.6.cloned.1.call-update) | async-done | bytes 1048592 | tf_op jit(solution)/shard_map/all_gather | solution.py:35
  188.6 1.7 multiply_add_fusion.17
  190.3 12.4 %all_gather.45 = f32[4,256,64]{1,2,0:T(8,128)S(1)} all-gather(f32[1,256,64]{1,2,0:T(8,128)S(1)} %get-tuple-element.32), channel_id=1, replica_groups=mesh['tm_0'=4,'tm_1'=16,'tm_2'=2,'space'=4] {'tm_0'}, dimensions={0}, use_global_device_ids=true | all-gather | bytes 327680 | tf_op jit(solution)/shard_map/all_gather | solution.py:35
  202.8 12.3 %all_gather.20 = f32[4,256,64]{1,2,0:T(8,128)S(1)} all-gather(f32[1,256,64]{1,2,0:T(8,128)S(1)} %slice_multiply_fusion.3), channel_id=1, replica_groups=mesh['tm_0'=4,'tm_1'=16,'tm_2'=2,'space'=4] {'tm_0'}, dimensions={0}, use_global_device_ids=true | all-gather | bytes 327680 | tf_op jit(solution)/shard_map/all_gather | solution.py:35
  218.6 1.9 collective-permute-start.1
  220.6 5.7 %collective-permute-done.1 = f32[256,64]{0,1:T(8,128)S(1)} collective-permute-done((f32[256,64]{0,1:T(8,128)S(1)}, f32[256,64]{0,1:T(8,128)S(1)}, u32[]{:S(2)}, u32[]{:S(2)}) %collective-permute-start.1) | collective-permute-done | bytes 65568 | tf_op jit(solution)/shard_map/ppermute | solution.py:21
  227.4 1.9 all_gather.46
  230.4 66.3 %all-gather.8.cloned.1.call-done = f32[16,256,64]{1,2,0:T(8,128)} async-done(((f32[1,256,64]{1,2,0:T(8,128)}), f32[16,256,64]{1,2,0:T(8,128)}) %all-gather.8.cloned.1.call-update) | async-done | bytes 1048592 | tf_op jit(solution)/shard_map/all_gather | solution.py:35
  298.1 12.4 %all_gather.48 = f32[4,256,64]{1,2,0:T(8,128)S(1)} all-gather(f32[1,256,64]{1,2,0:T(8,128)S(1)} %get-tuple-element.19), channel_id=1, replica_groups=mesh['tm_0'=4,'tm_1'=16,'tm_2'=2,'space'=4] {'tm_0'}, dimensions={0}, use_global_device_ids=true | all-gather | bytes 327680 | tf_op jit(solution)/shard_map/all_gather | solution.py:35
  312.5 2.1 fusion
  315.5 1.5 reshape.2403
  317.1 4.3 %all-to-all-start.1 = ((bf16[4,2,32768]{2,1,0:T(2,128)(2,1)}), bf16[4,2,32768]{2,1,0:T(2,128)(2,1)S(1)}, u32[]{:S(2)}, u32[]{:S(2)}) async-start(bf16[4,2,32768]{2,1,0:T(2,128)(2,1)} %reshape.2403), calls=%async_computation.1 | async-start | bytes 1048576 | tf_op jit(solution)/shard_map/all_to_all | solution.py:163
  321.4 11.0 %all-reduce = (f32[2,4]{1,0:T(2,128)S(1)}, f32[2,4]{1,0:T(2,128)S(1)}, f32[2,4]{1,0:T(2,128)S(1)}) all-reduce(f32[2,4]{1,0:T(2,128)S(1)} %pad_maximum_fusion.5, f32[2,4]{1,0:T(2,128)S(1)} %pad_maximum_fusion.6, f32[2,4]{1,0:T(2,128)S(1)} %pad_maximum_fusion.7), channel_id=1, replica_groups=mesh['tm_0'=4,'tm_1'=16,'tm_2'=2,'space'=4] {'space'}, use_global_device_ids=true, to_apply=%region_2.3 | all-reduce | flops 24 | bytes 192 | tf_op jit(solution)/shard_map/psum | solution.py:168
  335.2 2.3 fusion.59
  (111 shorter events, 21.4 us)
Async XLA Ops:
  12.2 14.4 %all-to-all-start = ((bf16[4,2,34816]{2,1,0:T(2,128)(2,1)}), bf16[4,2,34816]{2,1,0:T(2,128)(2,1)S(1)}, u32[]{:S(2)}, u32[]{:S(2)}) async-start(bf16[4,2,34816]{2,1,0:T(2,128)(2,1)} %reshape.2401), calls=%async_computation | async-start | bytes 1114112 | tf_op jit(solution)/shard_map/all_to_all | solution.py:84
  16.7 102.0 %all-gather.4.cloned.1.call-start = ((), (), s32[]{:S(2)}) async-start(), calls=%async_computation.2 | async-start | bytes 1114112 | tf_op jit(solution)/shard_map/all_gather | solution.py:35
  33.2 11.8 %copy-start.3 = (f32[17,256,64]{1,2,0:T(8,128)}, f32[17,256,64]{1,2,0:T(8,128)S(1)}, u32[]{:S(2)}) copy-start(f32[17,256,64]{1,2,0:T(8,128)S(1)} %convolution_bitcast_fusion) | copy-start | bytes 3342340
  33.3 2.1 copy-start.13
  33.5 11.5 %collective-permute-start = (f32[256,64]{0,1:T(8,128)S(1)}, f32[256,64]{0,1:T(8,128)S(1)}, u32[]{:S(2)}, u32[]{:S(2)}) collective-permute-start(f32[256,64]{0,1:T(8,128)S(1)} %slice_bitcast_fusion.7), channel_id=1, source_target_pairs={{0,4},{4,8},{8,12},{12,16},{16,20},{20,24},{24,28},{28,32},{32,36}... | collective-permute-start | bytes 196616 | tf_op jit(solution)/shard_map/ppermute | solution.py:21
  35.5 9.6 %copy-start.10 = (f32[1,256,64]{1,2,0:T(8,128)}, f32[1,256,64]{1,2,0:T(8,128)S(1)}, u32[]{:S(2)}) copy-start(f32[1,256,64]{1,2,0:T(8,128)S(1)} %bitcast_add_fusion.91) | copy-start | bytes 196612
  49.5 1.6 copy-start.6
  50.2 138.4 %all-gather.6.cloned.1.call-start = ((), (), s32[]{:S(2)}) async-start(), calls=%async_computation.3 | async-start | bytes 1114112 | tf_op jit(solution)/shard_map/all_gather | solution.py:35
  51.0 245.7 %all-gather.8.cloned.1.call-start = ((), (), s32[]{:S(2)}) async-start(), calls=%async_computation.4 | async-start | bytes 1114112 | tf_op jit(solution)/shard_map/all_gather | solution.py:35
  118.7 84.0 %copy-start = (f32[16,256,64]{1,2,0:T(8,128)S(1)}, f32[16,256,64]{1,2,0:T(8,128)}, u32[]{:S(2)}) copy-start(f32[16,256,64]{1,2,0:T(8,128)} %all-gather.4.cloned.1.call-done) | copy-start | bytes 3145732
  190.3 24.8 %copy-start.2 = (f32[16,256,64]{1,2,0:T(8,128)S(1)}, f32[16,256,64]{1,2,0:T(8,128)}, u32[]{:S(2)}) copy-start(f32[16,256,64]{1,2,0:T(8,128)} %all-gather.6.cloned.1.call-done) | copy-start | bytes 3145732
  190.3 24.8 %copy-start.7 = (f32[2,256,64]{1,2,0:T(8,128)S(1)}, f32[2,256,64]{1,2,0:T(8,128)}, u32[]{:S(2)}) copy-start(f32[2,256,64]{1,2,0:T(8,128)} %copy-done.6) | copy-start | bytes 393220
  190.3 24.8 %copy-start.14 = (f32[1,4,256,64]{2,3,1,0:T(8,128)S(1)}, f32[1,4,256,64]{2,3,1,0:T(8,128)}, u32[]{:S(2)}) copy-start(f32[1,4,256,64]{2,3,1,0:T(8,128)} %copy-done.13) | copy-start | bytes 786436
  190.3 24.8 %copy-start.16 = (f32[256,64]{0,1:T(8,128)S(1)}, f32[256,64]{0,1:T(8,128)}, u32[]{:S(2)}) copy-start(f32[256,64]{0,1:T(8,128)} %copy-done.15) | copy-start | bytes 196612
  215.8 11.4 %copy-start.4 = (f32[256,64]{0,1:T(8,128)}, f32[256,64]{0,1:T(8,128)S(1)}, u32[]{:S(2)}) copy-start(f32[256,64]{0,1:T(8,128)S(1)} %get-tuple-element.27) | copy-start | bytes 196612
  218.6 7.7 %collective-permute-start.1 = (f32[256,64]{0,1:T(8,128)S(1)}, f32[256,64]{0,1:T(8,128)S(1)}, u32[]{:S(2)}, u32[]{:S(2)}) collective-permute-start(f32[256,64]{0,1:T(8,128)S(1)} %slice_bitcast_fusion.6), channel_id=1, source_target_pairs={{0,4},{4,8},{8,12},{12,16},{16,20},{20,24},{24,28},{28,32},{32,36}... | collective-permute-start | bytes 196616 | tf_op jit(solution)/shard_map/ppermute | solution.py:21
  227.2 2.8 copy-start.12
  227.3 2.7 copy-start.5
  227.3 2.7 copy-start.17
  230.4 80.2 %copy-start.9 = (f32[4,256,64]{1,2,0:T(8,128)S(1)}, f32[4,256,64]{1,2,0:T(8,128)}, u32[]{:S(2)}) copy-start(f32[4,256,64]{1,2,0:T(8,128)} %copy-done.8) | copy-start | bytes 786436
  296.6 13.9 %copy-start.1 = (f32[16,256,64]{1,2,0:T(8,128)S(1)}, f32[16,256,64]{1,2,0:T(8,128)}, u32[]{:S(2)}) copy-start(f32[16,256,64]{1,2,0:T(8,128)} %all-gather.8.cloned.1.call-done) | copy-start | bytes 3145732
  315.5 5.9 %copy-start.24 = (f32[4]{0:T(128)S(1)}, f32[4]{0:T(128)}, u32[]{:S(2)}) copy-start(f32[4]{0:T(128)} %get-tuple-element.8) | copy-start | bytes 52
  315.5 5.9 %copy-start.23 = (f32[4]{0:T(128)S(1)}, f32[4]{0:T(128)}, u32[]{:S(2)}) copy-start(f32[4]{0:T(128)} %get-tuple-element.40) | copy-start | bytes 52
  317.1 15.9 %all-to-all-start.1 = ((bf16[4,2,32768]{2,1,0:T(2,128)(2,1)}), bf16[4,2,32768]{2,1,0:T(2,128)(2,1)S(1)}, u32[]{:S(2)}, u32[]{:S(2)}) async-start(bf16[4,2,32768]{2,1,0:T(2,128)(2,1)} %reshape.2403), calls=%async_computation.1 | async-start | bytes 1048576 | tf_op jit(solution)/shard_map/all_to_all | solution.py:163
  (8 other events, 6.6 us)
Sparse Core Ops, SparseCore 0:
  50.3 68.3 all-gather.3
  120.8 67.7 all-gather.5
  230.1 66.4 all-gather.7
where the time goes:
time: 345 us; the launch traced here: 344 us
  waiting for transfers between devices  229 us (66%)
  blocking collectives  53.8 us (16%)
  local copies, waits for them, and re-layouts  14.9 us (4%)
  between operations  14.3 us (4%)
  starting transfers between devices  12.7 us (4%)
  other arithmetic  11.9 us (3%)
  matrix products  7.08 us (2%)
    all_gather x3, waiting for transfers between devices, carried_in(): pieces = jax.tree.map(lambda part: lax.all_gather(part, axis), running)  204 us
    all_gather x6, blocking collectives, carried_in(): pieces = jax.tree.map(lambda part: lax.all_gather(part, axis), running)  42.8 us
    ppermute x2, waiting for transfers between devices, passed_along(): return lax.ppermute(block, axis, route)  15.2 us
    psum x1, blocking collectives, per_device(): lax.psum((jnp.stack(norm_rows), jnp.stack(corr_rows), jnp.stack(value_row...  11 us
    all_to_all x1, waiting for transfers between devices, per_device(): lax.all_to_all(halved, 'space', split_axis=2, concat_axis=1, tiled=True)  9.71 us
    unnamed x54, local copies, waits for them, and re-layouts  7.29 us
  transfers between devices with their start and end apart: 7, of which 6 were waited for; matrix products, arithmetic and copies ran while one was open for 0% of the time, Pallas kernels for 0%

commit v1 on v0

v1 whole, which is shorter than its diff:
```python
import math

import jax
import jax.numpy as jnp
import numpy as np
from jax import lax
from jax.experimental import pallas as pl
from jax.experimental.pallas import tpu as pltpu
from jax.sharding import Mesh
from jax.sharding import PartitionSpec as P

GRID = 256
NT = 2048
STEP = 0.004 / NT
X, Z, CORE, Y = "tm_0", "tm_1", "tm_2", "space"
NX, NZ = 4, 16
PHASES = 4
F32, BF16 = jnp.float32, jnp.bfloat16


def sine_tables():
    numbers = np.arange(1, GRID + 1)
    product = numbers[:, None] * numbers[None, :] % (2 * (GRID + 1))
    angles = (np.float32(np.pi) * product.astype(np.float32)) / np.float32(GRID + 1)
    table = (np.float32(math.sqrt(2.0 / (GRID + 1))) * np.sin(angles.astype(np.float64))).astype(np.float32)
    half = table.astype(jnp.bfloat16)
    rest = (table - half.astype(np.float32)).astype(jnp.bfloat16)
    return half, rest


def mode_tables():
    mu = (4.0 * (GRID + 1) ** 2 * np.sin(np.pi * np.arange(1, GRID + 1) / (2 * (GRID + 1))) ** 2).astype(np.float32)
    lane = np.arange(128)
    rows = np.broadcast_to(mu[:, None], (GRID, 128))
    packed = mu[64 * (lane // 32)[None, :] + np.arange(64)[:, None]]
    tiles = np.concatenate([packed.reshape(NZ, 4, 128)] * 2, axis=1)
    columns = np.broadcast_to(mu.reshape(8, 1, 32)[:, :, lane % 32], (8, 8, 128))
    return tuple(np.ascontiguousarray(t) for t in (rows, packed, tiles, columns))


def lane_group():
    return lax.broadcasted_iota(jnp.int32, (64, 128), 1) // 32


def turn(parts):
    group = lane_group()
    rolled = [parts[0]] + [pltpu.roll(parts[a], 32 * a, 1) for a in range(1, 4)]
    out = []
    for b in range(4):
        pick = [rolled[(g - b) % 4] for g in range(4)]
        mixed = jnp.where(
            group < 2, jnp.where(group == 0, pick[0], pick[1]), jnp.where(group == 2, pick[2], pick[3])
        )
        out.append(pltpu.roll(mixed, 128 - 32 * b, 1) if b else mixed)
    return out


def dot(a, b):
    return jnp.dot(a, b, preferred_element_type=F32)


class Weights:
    def __init__(self, x):
        one = 1.0
        gain = one / (one + x)
        y = 4.0 * x
        psi = one / (one + y)
        self.lift = lift = one + 16.0 * x
        theta = one / lift
        square = gain * gain
        phi = square * square
        psi2 = psi * psi
        psi3 = psi2 * psi
        psi4 = psi2 * psi2
        less = -(x * x * (6.0 + 4.0 * x + x * x)) * phi * psi
        deep = -(y * y * (6.0 + 4.0 * y + y * y)) * psi4 * theta
        big = phi * less
        alpha = 3.0 * big * psi2
        beta = psi3 * (big * psi3 + phi * deep)
        xb = psi3 * phi * lift
        c2 = psi4 * psi * big * phi - beta * xb
        c1 = 2.0 * big * phi * psi - alpha * xb
        kappa = (less * psi3 + deep) * lift
        bl2 = beta * lift * lift
        w1 = (phi * psi2, phi * psi, phi, xb)
        own = (psi4 * big * phi * lift, psi3 * big * phi * lift, None, (c1 + c2 * lift) * lift)
        w3 = tuple(bl2 * a if b is None else bl2 * a - b for a, b in zip(w1, own))
        self.w1 = w1
        self.w2 = (big * phi - w3[0], -w3[1], -w3[2], -w3[3])
        self.w3 = w3
        self.w4 = (less * phi * psi - kappa * w1[0], less * phi - kappa * w1[1], -kappa * w1[2], -kappa * w1[3])
        self.d2 = less * phi * psi2 - kappa * psi3 * phi
        self.e2 = -c2 * lift
        self.alpha = alpha + beta * lift
        self.gain, self.phi, self.psi, self.theta = gain, phi, psi, theta
        self.less, self.deep, self.xb, self.kappa = less, deep, xb, kappa


def weighted(weights, parts):
    total = weights[0] * parts[0]
    for w, part in zip(weights[1:], parts[1:]):
        total = total + w * part
    return total


def corrections(w, first, residual):
    out = []
    p, q = first, None
    for c in range(3):
        p = w.psi * p + residual[c]
        q = residual[c] if q is None else w.psi * q + residual[c]
        out.append(p)
    out.append(w.theta * first + (w.psi * q + residual[3]))
    return out


def kernel(
    forcing, starting, sine, sine_rest, mu_rows, mu_packed, mu_tiles, mu_columns,
    heat, history, change,
    fin, sin, sh, sr, mrow, mpack, mtile, mcol,
    send_a, recv_a, send_u, recv_u, start_c, src, send_n, recv_n,
    send_z, recv_z, send_x, recv_x, send_b, recv_b, send_o, recv_o, send_s, recv_s, hout,
    load_sem, store_sem, sa, ra, su, ru, sn, rn, sz, rz, sx, rx, sb, rb, so, ro, ss, rs,
):
    x, z, core, y = (lax.axis_index(a) for a in (X, Z, CORE, Y))
    me = 2 * y + core
    zn, zp = lax.rem(z + 1, NZ), lax.rem(z + NZ - 1, NZ)
    xn = jnp.where(z == NZ - 1, lax.rem(x + 1, NX), x)
    xp = jnp.where(z == 0, lax.rem(x + NX - 1, NX), x)
    my_rows = pl.ds(pl.multiple_of(64 * y, 64), 64)

    loads = [
        (forcing, fin), (sine, sh), (sine_rest, sr), (starting, sin), (mu_rows, mrow), (mu_packed, mpack),
        (mu_tiles.at[z], mtile), (mu_columns.at[me], mcol),
    ]
    loads = [pltpu.make_async_copy(a, b, load_sem.at[i]) for i, (a, b) in enumerate(loads)]
    for copy in loads:
        copy.start()

    barrier = pltpu.get_barrier_semaphore()
    for k in range(1, 8):
        d = lax.rem(me + k, 8)
        pl.semaphore_signal(barrier, inc=1, device_id={Y: d // 2, CORE: lax.rem(d, 2)})
    for k in range(1, NZ):
        pl.semaphore_signal(barrier, inc=1, device_id={Z: lax.rem(z + k, NZ)})
    for k in range(1, NX):
        pl.semaphore_signal(barrier, inc=1, device_id={X: lax.rem(x + k, NX)})
    pl.semaphore_signal(barrier, inc=1, device_id={X: xn, Z: zn})
    pl.semaphore_signal(barrier, inc=1, device_id={X: xp, Z: zp})

    loads[0].wait()
    loads[1].wait()
    table = sh[...]

    def halves(p):
        fields = jnp.concatenate([fin[4 * c + p] for c in range(4)], axis=0)
        product = dot(fields, table)
        for side in range(2):
            for q, part in enumerate(turn([product[64 * c : 64 * c + 64, 128 * side : 128 * side + 128] for c in range(4)])):
                send_a[p, 4 * side + q] = part.astype(BF16)

    def copy_a(p, d, source, from_core, rows):
        return pltpu.make_async_remote_copy(
            src_ref=send_a.at[p, d], dst_ref=recv_a.at[p, from_core, rows],
            send_sem=sa.at[p, d], recv_sem=ra.at[p, source], device_id={Y: d // 2, CORE: d % 2},
        )

    for p in range(PHASES):
        halves(p)
        if p == 0:
            pl.semaphore_wait(barrier, 27)
        for d in range(8):
            @pl.when(d != me)
            def _():
                copy_a(p, d, me, core, my_rows).start()

            @pl.when(d == me)
            def _():
                recv_a[p, core, my_rows] = send_a[p, d]

    first = jnp.logical_and(x == 0, z == 0)
    loads[3].wait()

    def copy_u(k, source):
        return pltpu.make_async_remote_copy(
            src_ref=send_u.at[k], dst_ref=recv_u.at[pl.ds(pl.multiple_of(64 * source, 64), 64)],
            send_sem=su.at[k], recv_sem=ru.at[source], device_id={Y: k},
        )

    @pl.when(first)
    def _():
        product = dot(sin[...], table)
        for k in range(4):
            side = product[:, 128 * (k // 2) : 128 * (k // 2) + 128]
            shift = 2 * (k % 2)
            even = pltpu.roll(side, (128 - 32 * shift) % 128, 1) if shift else side
            odd = pltpu.roll(side, (128 - 32 * (shift + 1)) % 128, 1)
            send_u[k] = jnp.where(core == 0, even, odd).astype(BF16)
        for k in range(4):
            @pl.when(k != y)
            def _():
                copy_u(k, y).start()

            @pl.when(k == y)
            def _():
                recv_u[my_rows] = send_u[k]

    for i in (2, 4, 5, 6, 7):
        loads[i].wait()
    gain = 1.0 / (1.0 + STEP * (mrow[...] + mcol[0:1, :]))
    w = Weights(STEP * (mpack[...] + mcol[0:1, :]))
    wo = Weights(STEP * (mtile[...] + mcol[...]))
    lower = lax.broadcasted_iota(jnp.int32, (8, 128), 0) < 4
    hop = wo.theta * wo.theta
    cross = jnp.where(lower, 0.0, 2.0 * wo.theta * wo.alpha)
    powers = [(jnp.ones_like(hop), jnp.zeros_like(hop))]
    for k in range(NZ):
        t, c = powers[-1]
        powers.append((hop * t, hop * c + cross * t))

    @pl.when(first)
    def _():
        for k in range(4):
            @pl.when(k != y)
            def _():
                copy_u(k, k).wait_recv()
        modes = dot(table, recv_u[...])
        group = lane_group()
        total = jnp.where(group == 0, modes[0:64], 0.0)
        for r in range(1, 4):
            total = jnp.where(group == r, pltpu.roll(modes[64 * r : 64 * r + 64], 32 * r, 1), total)
        start_c[...] = total

    @pl.when(jnp.logical_not(first))
    def _():
        start_c[...] = jnp.zeros_like(start_c)

    for p in range(PHASES):
        for s in range(8):
            @pl.when(s != me)
            def _():
                copy_a(p, s, s, s % 2, pl.ds(64 * (s // 2), 64)).wait_recv()
        for h in range(2):
            src[p, h] = gain * dot(table, recv_a[p, h])

    points = []
    for h in range(2):
        s = gain * src[0, h] + src[1, h]
        s = gain * s + src[2, h]
        s = gain * s + src[3, h]
        points.append(turn([s[64 * r : 64 * r + 64] for r in range(4)]))
    start = start_c[...]
    points[0][0] = points[0][0] + w.phi * start

    f = [weighted(w.w1, points[h]) for h in range(2)]
    g = [weighted(w.w2, points[h]) for h in range(2)]
    f_all = w.theta * f[0] + f[1]
    g_all = w.theta * g[0] + w.alpha * f[0] + g[1]
    for v in range(8):
        a, b = f_all[8 * v : 8 * v + 8], g_all[8 * v : 8 * v + 8]
        send_z[2 * v] = jnp.where(lower, a, pltpu.roll(b, 4, 0))
        send_z[2 * v + 1] = jnp.where(lower, pltpu.roll(a, 4, 0), b)

    def copy_z(to, source):
        return pltpu.make_async_remote_copy(
            src_ref=send_z.at[to], dst_ref=recv_z.at[source],
            send_sem=sz.at[to], recv_sem=rz.at[source], device_id={Z: to},
        )

    far_first = sorted(range(1, NZ), key=lambda k: -min(k, NZ - k))
    for k in far_first:
        copy_z(lax.rem(z + k, NZ), z).start()
    recv_z[z] = send_z[z]

    send_n[0] = points[1][3]
    send_n[1] = weighted(w.w4, points[1]) + w.d2 * points[0][3]
    send_n[2] = weighted(w.w3, points[1]) + w.e2 * points[0][3]
    copy_n = pltpu.make_async_remote_copy(
        src_ref=send_n, dst_ref=recv_n, send_sem=sn, recv_sem=rn, device_id={X: xn, Z: zn}
    )
    copy_n.start()

    for k in far_first[::-1]:
        source = lax.rem(z + k, NZ)
        copy_z(source, source).wait_recv()
    plain, coupled = [jnp.zeros((8, 128), F32)], [jnp.zeros((8, 128), F32)]
    for k in range(NZ):
        plain.append(hop * plain[-1] + recv_z[k])
    for k in range(NZ):
        coupled.append(hop * coupled[-1] + cross * pltpu.roll(plain[k], 4, 0))
    states = [a + b for a, b in zip(plain, coupled)]
    send_x[...] = states[NZ]

    def copy_x(to, source, k):
        return pltpu.make_async_remote_copy(
            src_ref=send_x, dst_ref=recv_x.at[source], send_sem=sx.at[k], recv_sem=rx.at[source], device_id={X: to}
        )

    for k in range(1, NX):
        copy_x(lax.rem(x + k, NX), x, k).start()
    for k in range(1, NX):
        source = lax.rem(x + k, NX)
        copy_x(source, source, k).wait_recv()
    recv_x[x] = states[NZ]
    entering = jnp.zeros((8, 128), F32)
    for k in range(NX - 1):
        further = powers[NZ][0] * entering + powers[NZ][1] * pltpu.roll(entering, 4, 0) + recv_x[k]
        entering = jnp.where(k < x, further, entering)
    turned = pltpu.roll(entering, 4, 0)
    for k in range(NZ):
        send_b[k] = states[k] + (powers[k][0] * entering + powers[k][1] * turned)

    def copy_b(to, source):
        return pltpu.make_async_remote_copy(
            src_ref=send_b.at[to], dst_ref=recv_b.at[source],
            send_sem=sb.at[to], recv_sem=rb.at[source], device_id={Z: to},
        )

    for k in far_first:
        copy_b(lax.rem(z + k, NZ), z).start()
    recv_b[z] = send_b[z]

    copy_n.wait_recv()
    keep = jnp.logical_not(first)
    near = [jnp.where(keep, recv_n[i], 0.0) for i in range(3)]
    residual_a = [near[0], points[0][3]]
    near_d = [near[1], weighted(w.w4, points[0]) + w.d2 * near[0]]
    near_e = [near[2], weighted(w.w3, points[0]) + w.e2 * near[0]]

    for k in far_first[::-1]:
        source = lax.rem(z + k, NZ)
        copy_b(source, source).wait_recv()
    fs, gs = [], []
    for v in range(8):
        a, b = recv_b[2 * v], recv_b[2 * v + 1]
        fs.append(jnp.where(lower, a, pltpu.roll(b, 4, 0)))
        gs.append(jnp.where(lower, pltpu.roll(a, 4, 0), b))
    f_in = jnp.concatenate(fs, axis=0)
    g_in = jnp.concatenate(gs, axis=0)

    sums = []
    for h in range(2):
        if h == 1:
            g_in = w.theta * g_in + w.alpha * f_in + g[0]
            f_in = w.theta * f_in + f[0]
        s = points[h]
        a = residual_a[h]
        e1 = f_in - w.xb * a
        d = w.kappa * f_in + near_d[h]
        e2 = g_in + near_e[h]
        r1 = [w.phi * a] + [w.phi * s[c] for c in range(3)]
        p1 = corrections(w, e1, r1)
        later = [w.less * e1, w.less * p1[0], w.less * p1[1], w.less * p1[2] + w.deep * e1]
        r2 = [w.phi * d] + [w.phi * later[c] for c in range(3)]
        p2 = corrections(w, e2, r2)
        v1 = [s[c] + p1[c] for c in range(4)]
        v2 = [v1[c] + later[c] + p2[c] for c in range(4)]
        enter = a + e1 + d + e2
        if h == 0:
            enter = enter + start
        squares = [jnp.sum(q * q, axis=0, keepdims=True) for q in r1 + r2 + p1 + p2 + v1 + v2]
        sums.append(squares)
        begin = jnp.concatenate(turn([enter, v2[0], v2[1], v2[2]]), axis=0)
        ends = jnp.concatenate(turn(v2), axis=0)
        u = begin
        for p in range(3):
            u = gain * u + src[p, h]
            src[p, h] = u
        src[3, h] = ends

    def copy_o(p, h, k, source):
        return pltpu.make_async_remote_copy(
            src_ref=send_o.at[p, h, pl.ds(64 * k, 64)], dst_ref=recv_o.at[p, source],
            send_sem=so.at[p, h, k], recv_sem=ro.at[p, source], device_id={Y: k, CORE: h},
        )

    rest = sr[...]
    for p in range(PHASES):
        for h in range(2):
            u = src[p, h]
            high = u.astype(BF16)
            low = (u - high.astype(F32)).astype(BF16)
            send_o[p, h] = (dot(table, high) + (dot(table, low) + dot(rest, high))).astype(BF16)
        for h in range(2):
            for k in range(4):
                @pl.when(2 * k + h != me)
                def _():
                    copy_o(p, h, k, me).start()

                @pl.when(2 * k + h == me)
                def _():
                    recv_o[p, me] = send_o[p, h, 64 * k : 64 * k + 64]

    def copy_s(h, k, source):
        return pltpu.make_async_remote_copy(
            src_ref=send_s.at[h], dst_ref=recv_s.at[source],
            send_sem=ss.at[h, k], recv_sem=rs.at[source], device_id={Y: k, CORE: h},
        )

    for h in range(2):
        send_s[h] = jnp.concatenate(sums[h], axis=0)
    for h in range(2):
        for k in range(4):
            @pl.when(2 * k + h != me)
            def _():
                copy_s(h, k, me).start()

            @pl.when(2 * k + h == me)
            def _():
                recv_s[me] = send_s[h]

    stores = []
    for p in range(PHASES):
        for s in range(8):
            @pl.when(s != me)
            def _():
                copy_o(p, s % 2, s // 2, s).wait_recv()
        sides = []
        for side in range(2):
            sides.append(turn([recv_o[p, 4 * side + q].astype(F32) for q in range(4)]))
        rows = jnp.concatenate(
            [jnp.concatenate([sides[0][c], sides[1][c]], axis=1) for c in range(4)], axis=0
        ).astype(BF16)
        field = dot(rows, table)
        for c in range(4):
            hout[4 * c + p] = field[64 * c : 64 * c + 64]
            stores.append(pltpu.make_async_copy(hout.at[4 * c + p], heat.at[4 * c + p], store_sem.at[4 * c + p]))
            stores[-1].start()

    for s in range(8):
        @pl.when(s != me)
        def _():
            copy_s(s % 2, s // 2, s).wait_recv()
    total = recv_s[0]
    for s in range(1, 8):
        total = total + recv_s[s]
    total = jnp.sum(total, axis=1, keepdims=True)
    norms = jnp.sqrt(total[0:8] / (GRID * GRID))
    ratios = jnp.sqrt(total[8:16] / total[16:24])
    mine = lax.broadcasted_iota(jnp.int32, (8, 128), 1) == lax.broadcasted_iota(jnp.int32, (8, 128), 0) % 4
    for column, out in ((norms, history), (ratios, change)):
        spread = jnp.where(mine, column, 0.0)
        for i in range(2):
            out[i : i + 1, :] = jnp.sum(spread[4 * i : 4 * i + 4], axis=0, keepdims=True)[:, 0:4]

    for p in range(PHASES):
        for d in range(8):
            @pl.when(d != me)
            def _():
                copy_a(p, d, me, core, my_rows).wait_send()
                copy_o(p, d % 2, d // 2, me).wait_send()

    for d in range(8):
        @pl.when(d != me)
        def _():
            copy_s(d % 2, d // 2, me).wait_send()

    @pl.when(first)
    def _():
        for k in range(4):
            @pl.when(k != y)
            def _():
                copy_u(k, y).wait_send()

    copy_n.wait_send()
    for k in range(1, NZ):
        to = lax.rem(z + k, NZ)
        copy_z(to, z).wait_send()
        copy_b(to, z).wait_send()
    for k in range(1, NX):
        copy_x(lax.rem(x + k, NX), x, k).wait_send()
    for copy in stores:
        copy.wait()


def per_device(forcing, starting_heat):
    half, rest = sine_tables()
    tables = mode_tables()
    anywhere = pl.BlockSpec(memory_space=pl.ANY)
    vmem = pl.BlockSpec(memory_space=pltpu.VMEM)
    dma = pltpu.SemaphoreType.DMA
    scratch = [
        pltpu.VMEM((16, 64, 256), BF16), pltpu.VMEM((64, 256), BF16),
        pltpu.VMEM((256, 256), BF16), pltpu.VMEM((256, 256), BF16),
        pltpu.VMEM((256, 128), F32), pltpu.VMEM((64, 128), F32),
        pltpu.VMEM((8, 128), F32), pltpu.VMEM((8, 128), F32),
        pltpu.VMEM((4, 8, 64, 128), BF16), pltpu.VMEM((4, 2, 256, 128), BF16),
        pltpu.VMEM((4, 64, 128), BF16), pltpu.VMEM((256, 128), BF16), pltpu.VMEM((64, 128), F32),
        pltpu.VMEM((4, 2, 256, 128), F32), pltpu.VMEM((3, 64, 128), F32), pltpu.VMEM((3, 64, 128), F32),
        pltpu.VMEM((16, 8, 128), F32), pltpu.VMEM((16, 8, 128), F32),
        pltpu.VMEM((8, 128), F32), pltpu.VMEM((4, 8, 128), F32),
        pltpu.VMEM((16, 8, 128), F32), pltpu.VMEM((16, 8, 128), F32),
        pltpu.VMEM((4, 2, 256, 128), BF16), pltpu.VMEM((4, 8, 64, 128), BF16),
        pltpu.VMEM((2, 24, 128), F32), pltpu.VMEM((8, 24, 128), F32),
        pltpu.VMEM((16, 64, 256), F32),
        dma((8,)), dma((16,)), dma((4, 8)), dma((4, 8)), dma((4,)), dma((4,)), dma, dma,
        dma((16,)), dma((16,)), dma((4,)), dma((4,)), dma((16,)), dma((16,)),
        dma((4, 2, 4)), dma((4, 8)), dma((2, 4)), dma((8,)),
    ]
    return pl.pallas_call(
        kernel,
        out_shape=(
            jax.ShapeDtypeStruct((16, 64, 256), F32),
            jax.ShapeDtypeStruct((2, 4), F32),
            jax.ShapeDtypeStruct((2, 4), F32),
        ),
        in_specs=[anywhere] * 8,
        out_specs=(anywhere, vmem, vmem),
        scratch_shapes=scratch,
        compiler_params=pltpu.CompilerParams(collective_id=0, has_side_effects=True),
    )(forcing, starting_heat, half, rest, *tables)


def solution(mesh):
    torus = Mesh(mesh.devices.reshape(NX, NZ, 2, mesh.shape["space"]), (X, Z, CORE, Y))
    times = (X, Z, CORE)
    in_specs = (P(times, Y, None), P(Y, None))
    out_specs = (P(times, Y, None), P(None, times), P(None, times))
    return jax.shard_map(per_device, mesh=torus, in_specs=in_specs, out_specs=out_specs, check_vma=False)
```

time: 345 us -> 59.3 us (0.17)
  the two profiles are of different devices: /device:TPU:2 before, /device:TPU:1 now
where the time goes in v1:
time: 59.3 us; the launch traced here: 59.1 us
  Pallas kernels  54.9 us (93%)
  local copies, waits for them, and re-layouts  3.52 us (6%)
  between operations  0.65 us (1%)
    pallas_call x1, Pallas kernels, per_device(): pl.pallas_call(kernel, out_shape=(jax.ShapeDtypeStruct((16, 64, 256), F32...  54.9 us
    unnamed x7, local copies, waits for them, and re-layouts  3.52 us

profile of v1, /device:TPU:1, one launch (start us, length us, event | category | flops | bytes accessed | tf_op | source)
XLA Modules:
  0.0 59.1 jit_solution(1986211167655172226)
XLA Ops:
  0.6 54.9 %shard_map.103 = (f32[16,64,256]{2,1,0:T(8,128)}, f32[2,4]{1,0:T(2,128)}, f32[2,4]{1,0:T(2,128)}) custom-call(bf16[16,64,256]{2,1,0:T(8,128)(2,1)} %forcing.1, bf16[64,256]{1,0:T(8,128)(2,1)} %starting.1, bf16[256,256]{1,0:T(8,128)(2,1)} %constant.12.clone.sine, bf16[256,256]{1,0:T(8,128)(2,1)} %constant.13.clone.sine_rest, ...), custom_call_target="tpu_custom_call" | custom-call | tf_op jit(solution)/shard_map/pallas_call | solution.py:500
  55.6 0.0 copy-start.1
  55.6 2.3 %copy.14 = f32[16,64,256]{2,1,0:T(8,128)} copy(f32[16,64,256]{2,1,0:T(8,128)} %get-tuple-element.6) | data formatting | bytes 2097152
  57.9 0.0 copy-done.1
  57.9 0.0 copy-start
  57.9 0.6 copy.15
  58.4 0.1 copy-done
  58.5 0.6 copy.16
Async XLA Ops:
  55.6 2.3 %copy-start.1 = (f32[2,4]{1,0:T(2,128)S(1)}, f32[2,4]{1,0:T(2,128)}, u32[]{:S(2)}) copy-start(f32[2,4]{1,0:T(2,128)} %get-tuple-element.7) | copy-start | bytes 100
  57.9 0.7 %copy-start = (f32[2,4]{1,0:T(2,128)S(1)}, f32[2,4]{1,0:T(2,128)}, u32[]{:S(2)}) copy-start(f32[2,4]{1,0:T(2,128)} %get-tuple-element.8) | copy-start | bytes 100

commit v2 on v1

--- a/solution.py
+++ b/solution.py
@@ -116,11 +116,11 @@
 
 def kernel(
     forcing, starting, sine, sine_rest, mu_rows, mu_packed, mu_tiles, mu_columns,
-    heat, history, change,
+    recv_o, recv_s,
     fin, sin, sh, sr, mrow, mpack, mtile, mcol,
     send_a, recv_a, send_u, recv_u, start_c, src, send_n, recv_n,
-    send_z, recv_z, send_x, recv_x, send_b, recv_b, send_o, recv_o, send_s, recv_s, hout,
-    load_sem, store_sem, sa, ra, su, ru, sn, rn, sz, rz, sx, rx, sb, rb, so, ro, ss, rs,
+    send_z, recv_z, send_x, recv_x, send_b, recv_b, send_o, send_s,
+    load_sem, own_sem, met, sa, ra, su, ru, sn, rn, sz, rz, sx, rx, sb, rb, so, ro, ss, rs,
 ):
     x, z, core, y = (lax.axis_index(a) for a in (X, Z, CORE, Y))
     me = 2 * y + core
@@ -129,6 +129,17 @@
     xp = jnp.where(z == 0, lax.rem(x + NX - 1, NX), x)
     my_rows = pl.ds(pl.multiple_of(64 * y, 64), 64)
 
+    barrier = pltpu.get_barrier_semaphore()
+    for k in range(1, 8):
+        d = lax.rem(me + k, 8)
+        pl.semaphore_signal(barrier, inc=1, device_id={Y: d // 2, CORE: lax.rem(d, 2)})
+    pl.semaphore_signal(barrier, inc=1, device_id={Z: zn})
+    pl.semaphore_signal(barrier, inc=1, device_id={Z: zp})
+    for k in range(1, NX):
+        pl.semaphore_signal(barrier, inc=1, device_id={X: lax.rem(x + k, NX)})
+    pl.semaphore_signal(barrier, inc=1, device_id={X: xn, Z: zn})
+    pl.semaphore_signal(barrier, inc=1, device_id={X: xp, Z: zp})
+
     loads = [
         (forcing, fin), (sine, sh), (sine_rest, sr), (starting, sin), (mu_rows, mrow), (mu_packed, mpack),
         (mu_tiles.at[z], mtile), (mu_columns.at[me], mcol),
@@ -137,16 +148,9 @@
     for copy in loads:
         copy.start()
 
-    barrier = pltpu.get_barrier_semaphore()
-    for k in range(1, 8):
-        d = lax.rem(me + k, 8)
-        pl.semaphore_signal(barrier, inc=1, device_id={Y: d // 2, CORE: lax.rem(d, 2)})
-    for k in range(1, NZ):
-        pl.semaphore_signal(barrier, inc=1, device_id={Z: lax.rem(z + k, NZ)})
-    for k in range(1, NX):
-        pl.semaphore_signal(barrier, inc=1, device_id={X: lax.rem(x + k, NX)})
-    pl.semaphore_signal(barrier, inc=1, device_id={X: xn, Z: zn})
-    pl.semaphore_signal(barrier, inc=1, device_id={X: xp, Z: zp})
+    def greet(r):
+        for k in (2**r, NZ - 2**r):
+            pl.semaphore_signal(met.at[r], inc=1, device_id={Z: lax.rem(z + k, NZ)})
 
     loads[0].wait()
     loads[1].wait()
@@ -168,7 +172,8 @@
     for p in range(PHASES):
         halves(p)
         if p == 0:
-            pl.semaphore_wait(barrier, 27)
+            pl.semaphore_wait(barrier, 14)
+            greet(0)
         for d in range(8):
             @pl.when(d != me)
             def _():
@@ -218,6 +223,9 @@
         t, c = powers[-1]
         powers.append((hop * t, hop * c + cross * t))
 
+    pl.semaphore_wait(met.at[0], 2)
+    greet(1)
+
     @pl.when(first)
     def _():
         for k in range(4):
@@ -240,6 +248,9 @@
             @pl.when(s != me)
             def _():
                 copy_a(p, s, s, s % 2, pl.ds(64 * (s // 2), 64)).wait_recv()
+        if p == 0:
+            pl.semaphore_wait(met.at[1], 2)
+            greet(2)
         for h in range(2):
             src[p, h] = gain * dot(table, recv_a[p, h])
 
@@ -267,6 +278,7 @@
             send_sem=sz.at[to], recv_sem=rz.at[source], device_id={Z: to},
         )
 
+    pl.semaphore_wait(met.at[2], 2)
     far_first = sorted(range(1, NZ), key=lambda k: -min(k, NZ - k))
     for k in far_first:
         copy_z(lax.rem(z + k, NZ), z).start()
@@ -374,6 +386,12 @@
             send_sem=so.at[p, h, k], recv_sem=ro.at[p, source], device_id={Y: k, CORE: h},
         )
 
+    def keep_o(p, h, k):
+        return pltpu.make_async_copy(send_o.at[p, h, pl.ds(64 * k, 64)], recv_o.at[p, me], own_sem.at[p])
+
+    def keep_s(h):
+        return pltpu.make_async_copy(send_s.at[h], recv_s.at[me], own_sem.at[4])
+
     rest = sr[...]
     for p in range(PHASES):
         for h in range(2):
@@ -389,7 +407,7 @@
 
                 @pl.when(2 * k + h == me)
                 def _():
-                    recv_o[p, me] = send_o[p, h, 64 * k : 64 * k + 64]
+                    keep_o(p, h, k).start()
 
     def copy_s(h, k, source):
         return pltpu.make_async_remote_copy(
@@ -407,53 +425,36 @@
 
             @pl.when(2 * k + h == me)
             def _():
-                recv_s[me] = send_s[h]
-
-    stores = []
+                keep_s(h).start()
+
     for p in range(PHASES):
         for s in range(8):
             @pl.when(s != me)
             def _():
                 copy_o(p, s % 2, s // 2, s).wait_recv()
-        sides = []
-        for side in range(2):
-            sides.append(turn([recv_o[p, 4 * side + q].astype(F32) for q in range(4)]))
-        rows = jnp.concatenate(
-            [jnp.concatenate([sides[0][c], sides[1][c]], axis=1) for c in range(4)], axis=0
-        ).astype(BF16)
-        field = dot(rows, table)
-        for c in range(4):
-            hout[4 * c + p] = field[64 * c : 64 * c + 64]
-            stores.append(pltpu.make_async_copy(hout.at[4 * c + p], heat.at[4 * c + p], store_sem.at[4 * c + p]))
-            stores[-1].start()
-
     for s in range(8):
         @pl.when(s != me)
         def _():
             copy_s(s % 2, s // 2, s).wait_recv()
-    total = recv_s[0]
-    for s in range(1, 8):
-        total = total + recv_s[s]
-    total = jnp.sum(total, axis=1, keepdims=True)
-    norms = jnp.sqrt(total[0:8] / (GRID * GRID))
-    ratios = jnp.sqrt(total[8:16] / total[16:24])
-    mine = lax.broadcasted_iota(jnp.int32, (8, 128), 1) == lax.broadcasted_iota(jnp.int32, (8, 128), 0) % 4
-    for column, out in ((norms, history), (ratios, change)):
-        spread = jnp.where(mine, column, 0.0)
-        for i in range(2):
-            out[i : i + 1, :] = jnp.sum(spread[4 * i : 4 * i + 4], axis=0, keepdims=True)[:, 0:4]
-
     for p in range(PHASES):
         for d in range(8):
             @pl.when(d != me)
             def _():
                 copy_a(p, d, me, core, my_rows).wait_send()
                 copy_o(p, d % 2, d // 2, me).wait_send()
+
+            @pl.when(d == me)
+            def _():
+                keep_o(p, d % 2, d // 2).wait()
 
     for d in range(8):
         @pl.when(d != me)
         def _():
             copy_s(d % 2, d // 2, me).wait_send()
+
+        @pl.when(d == me)
+        def _():
+            keep_s(d % 2).wait()
 
     @pl.when(first)
     def _():
@@ -469,15 +470,38 @@
         copy_b(to, z).wait_send()
     for k in range(1, NX):
         copy_x(lax.rem(x + k, NX), x, k).wait_send()
-    for copy in stores:
-        copy.wait()
+
+
+def finish(rows, squares, sine, heat, history, change):
+    sides = []
+    for side in range(2):
+        sides.append(turn([rows[0, 4 * side + q].astype(F32) for q in range(4)]))
+    stacked = jnp.concatenate(
+        [jnp.concatenate([sides[0][c], sides[1][c]], axis=1) for c in range(4)], axis=0
+    ).astype(BF16)
+    field = dot(stacked, sine[...])
+    for c in range(4):
+        heat[c, 0] = field[64 * c : 64 * c + 64]
+
+    @pl.when(pl.program_id(0) == 0)
+    def _():
+        total = squares[0]
+        for s in range(1, 8):
+            total = total + squares[s]
+        total = jnp.sum(total, axis=1, keepdims=True)
+        norms = jnp.sqrt(total[0:8] / (GRID * GRID))
+        ratios = jnp.sqrt(total[8:16] / total[16:24])
+        mine = lax.broadcasted_iota(jnp.int32, (8, 128), 1) == lax.broadcasted_iota(jnp.int32, (8, 128), 0) % 4
+        for column, out in ((norms, history), (ratios, change)):
+            spread = jnp.where(mine, column, 0.0)
+            for i in range(2):
+                out[i : i + 1, :] = jnp.sum(spread[4 * i : 4 * i + 4], axis=0, keepdims=True)[:, 0:4]
 
 
 def per_device(forcing, starting_heat):
     half, rest = sine_tables()
     tables = mode_tables()
     anywhere = pl.BlockSpec(memory_space=pl.ANY)
-    vmem = pl.BlockSpec(memory_space=pltpu.VMEM)
     dma = pltpu.SemaphoreType.DMA
     scratch = [
         pltpu.VMEM((16, 64, 256), BF16), pltpu.VMEM((64, 256), BF16),
@@ -490,25 +514,39 @@
         pltpu.VMEM((16, 8, 128), F32), pltpu.VMEM((16, 8, 128), F32),
         pltpu.VMEM((8, 128), F32), pltpu.VMEM((4, 8, 128), F32),
         pltpu.VMEM((16, 8, 128), F32), pltpu.VMEM((16, 8, 128), F32),
-        pltpu.VMEM((4, 2, 256, 128), BF16), pltpu.VMEM((4, 8, 64, 128), BF16),
-        pltpu.VMEM((2, 24, 128), F32), pltpu.VMEM((8, 24, 128), F32),
-        pltpu.VMEM((16, 64, 256), F32),
-        dma((8,)), dma((16,)), dma((4, 8)), dma((4, 8)), dma((4,)), dma((4,)), dma, dma,
+        pltpu.VMEM((4, 2, 256, 128), BF16), pltpu.VMEM((2, 24, 128), F32),
+        dma((8,)), dma((5,)), pltpu.SemaphoreType.REGULAR((3,)), dma((4, 8)), dma((4, 8)), dma((4,)), dma((4,)), dma, dma,
         dma((16,)), dma((16,)), dma((4,)), dma((4,)), dma((16,)), dma((16,)),
         dma((4, 2, 4)), dma((4, 8)), dma((2, 4)), dma((8,)),
     ]
-    return pl.pallas_call(
+    rows, squares = pl.pallas_call(
         kernel,
+        out_shape=(jax.ShapeDtypeStruct((4, 8, 64, 128), BF16), jax.ShapeDtypeStruct((8, 24, 128), F32)),
+        in_specs=[anywhere] * 8,
+        out_specs=(anywhere, anywhere),
+        scratch_shapes=scratch,
+        compiler_params=pltpu.CompilerParams(collective_id=0, has_side_effects=True),
+    )(forcing, starting_heat, half, rest, *tables)
+    heat, history, change = pl.pallas_call(
+        finish,
+        grid=(PHASES,),
         out_shape=(
-            jax.ShapeDtypeStruct((16, 64, 256), F32),
+            jax.ShapeDtypeStruct((4, PHASES, 64, 256), F32),
             jax.ShapeDtypeStruct((2, 4), F32),
             jax.ShapeDtypeStruct((2, 4), F32),
         ),
-        in_specs=[anywhere] * 8,
-        out_specs=(anywhere, vmem, vmem),
-        scratch_shapes=scratch,
-        compiler_params=pltpu.CompilerParams(collective_id=0, has_side_effects=True),
-    )(forcing, starting_heat, half, rest, *tables)
+        in_specs=[
+            pl.BlockSpec((1, 8, 64, 128), lambda p: (p, 0, 0, 0)),
+            pl.BlockSpec((8, 24, 128), lambda p: (0, 0, 0)),
+            pl.BlockSpec((256, 256), lambda p: (0, 0)),
+        ],
+        out_specs=(
+            pl.BlockSpec((4, 1, 64, 256), lambda p: (0, p, 0, 0)),
+            pl.BlockSpec((2, 4), lambda p: (0, 0)),
+            pl.BlockSpec((2, 4), lambda p: (0, 0)),
+        ),
+    )(rows, squares, half)
+    return heat.reshape(forcing.shape), history, change
 
 
 def solution(mesh):

time: 59.3 us -> 54.8 us (0.924)
  local copies, waits for them, and re-layouts: 3.52 us -> 0 us
  Pallas kernels: 54.9 us -> 53.9 us
    unnamed x7 -> x0, local copies, waits for them, and re-layouts: 3.52 us -> none
    pallas_call x1 -> x2, Pallas kernels: 54.9 us -> 53.9 us  [the longest x1 49.9 us: per_device(): pl.pallas_call(kernel, out_shape=(jax.ShapeDtypeStruct((4, 8, 64, 128), B...]
where the time goes in v2:
time: 54.8 us; the launch traced here: 54.6 us
  Pallas kernels  53.9 us (98%)
  between operations  0.64 us (1%)
    pallas_call x1, Pallas kernels, per_device(): pl.pallas_call(kernel, out_shape=(jax.ShapeDtypeStruct((4, 8, 64, 128), B...  49.9 us
    pallas_call x1, Pallas kernels, per_device(): pl.pallas_call(finish, grid=(PHASES,), out_shape=(jax.ShapeDtypeStruct((4...  4.05 us

profile of v2, /device:TPU:1, one launch (start us, length us, event | category | flops | bytes accessed | tf_op | source)
XLA Modules:
  0.0 54.6 jit_solution(14353786745664258254)
XLA Ops:
  0.6 49.9 %shard_map.103 = (bf16[4,8,64,128]{3,2,1,0:T(8,128)(2,1)}, f32[8,24,128]{2,1,0:T(8,128)}) custom-call(bf16[16,64,256]{2,1,0:T(8,128)(2,1)} %forcing.1, bf16[64,256]{1,0:T(8,128)(2,1)} %starting.1, bf16[256,256]{1,0:T(8,128)(2,1)} %constant.12.clone.sine, bf16[256,256]{1,0:T(8,128)(2,1)} %constant.13.clone.sine_rest, f32[256,128]{1,0:T(8,128)} %constant.14.clone.mu_rows, ...), custom_call_target="tpu_custom_call" | custom-call | tf_op jit(solution)/shard_map/pallas_call | solution.py:522
  50.5 4.0 %shard_map.104 = (f32[4,4,64,256]{3,2,1,0:T(8,128)}, f32[2,4]{1,0:T(2,128)}, f32[2,4]{1,0:T(2,128)}) custom-call(bf16[4,8,64,128]{3,2,1,0:T(8,128)(2,1)} %get-tuple-element.8.rows, f32[8,24,128]{2,1,0:T(8,128)} %get-tuple-element.9.squares, bf16[256,256]{1,0:T(8,128)(2,1)} %constant.12.clone.sine), custom_call_target="tpu_custom_call" | custom-call | tf_op jit(solution)/shard_map/pallas_call | solution.py:530

commit v3 on v1

--- a/solution.py
+++ b/solution.py
@@ -57,6 +57,10 @@
 
 def dot(a, b):
     return jnp.dot(a, b, preferred_element_type=F32)
+
+
+def taken(sem, ref):
+    pltpu.make_async_copy(ref, ref, sem).wait()
 
 
 class Weights:
@@ -116,11 +120,11 @@
 
 def kernel(
     forcing, starting, sine, sine_rest, mu_rows, mu_packed, mu_tiles, mu_columns,
-    heat, history, change,
+    hout, history, change,
     fin, sin, sh, sr, mrow, mpack, mtile, mcol,
     send_a, recv_a, send_u, recv_u, start_c, src, send_n, recv_n,
-    send_z, recv_z, send_x, recv_x, send_b, recv_b, send_o, recv_o, send_s, recv_s, hout,
-    load_sem, store_sem, sa, ra, su, ru, sn, rn, sz, rz, sx, rx, sb, rb, so, ro, ss, rs,
+    send_z, recv_z, send_x, recv_x, send_b, recv_b, send_o, recv_o, send_s, recv_s,
+    load_sem, met, sa, ra, su, ru, sn, rn, sz, rz, sx, rx, sb, rb, so, ro, ss, rs,
 ):
     x, z, core, y = (lax.axis_index(a) for a in (X, Z, CORE, Y))
     me = 2 * y + core
@@ -129,62 +133,71 @@
     xp = jnp.where(z == 0, lax.rem(x + NX - 1, NX), x)
     my_rows = pl.ds(pl.multiple_of(64 * y, 64), 64)
 
-    loads = [
-        (forcing, fin), (sine, sh), (sine_rest, sr), (starting, sin), (mu_rows, mrow), (mu_packed, mpack),
-        (mu_tiles.at[z], mtile), (mu_columns.at[me], mcol),
-    ]
-    loads = [pltpu.make_async_copy(a, b, load_sem.at[i]) for i, (a, b) in enumerate(loads)]
-    for copy in loads:
-        copy.start()
-
     barrier = pltpu.get_barrier_semaphore()
     for k in range(1, 8):
         d = lax.rem(me + k, 8)
         pl.semaphore_signal(barrier, inc=1, device_id={Y: d // 2, CORE: lax.rem(d, 2)})
-    for k in range(1, NZ):
-        pl.semaphore_signal(barrier, inc=1, device_id={Z: lax.rem(z + k, NZ)})
+    pl.semaphore_signal(barrier, inc=1, device_id={Z: zn})
+    pl.semaphore_signal(barrier, inc=1, device_id={Z: zp})
     for k in range(1, NX):
         pl.semaphore_signal(barrier, inc=1, device_id={X: lax.rem(x + k, NX)})
     pl.semaphore_signal(barrier, inc=1, device_id={X: xn, Z: zn})
     pl.semaphore_signal(barrier, inc=1, device_id={X: xp, Z: zp})
 
+    loads = [
+        (sine, sh), (sine_rest, sr), (starting, sin), (mu_rows, mrow), (mu_packed, mpack), (mu_tiles.at[z], mtile),
+        (mu_columns.at[me], mcol),
+    ]
+    loads = [pltpu.make_async_copy(a, b, load_sem.at[i]) for i, (a, b) in enumerate(loads)]
+    loads[0].start()
+    for p in range(PHASES):
+        for c in range(4):
+            pltpu.make_async_copy(forcing.at[4 * c + p], fin.at[p, c], load_sem.at[7 + p]).start()
+
+    def greet(r):
+        for k in (2**r, NZ - 2**r):
+            pl.semaphore_signal(met.at[r], inc=1, device_id={Z: lax.rem(z + k, NZ)})
+
     loads[0].wait()
-    loads[1].wait()
     table = sh[...]
 
     def halves(p):
-        fields = jnp.concatenate([fin[4 * c + p] for c in range(4)], axis=0)
-        product = dot(fields, table)
+        product = dot(fin[p].reshape(256, 256), table)
         for side in range(2):
             for q, part in enumerate(turn([product[64 * c : 64 * c + 64, 128 * side : 128 * side + 128] for c in range(4)])):
                 send_a[p, 4 * side + q] = part.astype(BF16)
 
-    def copy_a(p, d, source, from_core, rows):
-        return pltpu.make_async_remote_copy(
-            src_ref=send_a.at[p, d], dst_ref=recv_a.at[p, from_core, rows],
-            send_sem=sa.at[p, d], recv_sem=ra.at[p, source], device_id={Y: d // 2, CORE: d % 2},
+    def copy_a(p, d):
+        return pltpu.make_async_remote_copy(
+            src_ref=send_a.at[p, d], dst_ref=recv_a.at[p, core, my_rows],
+            send_sem=sa, recv_sem=ra.at[p], device_id={Y: d // 2, CORE: d % 2},
         )
 
     for p in range(PHASES):
+        taken(load_sem.at[7 + p], fin.at[p])
+        if p == 0:
+            for copy in loads[1:]:
+                copy.start()
         halves(p)
         if p == 0:
-            pl.semaphore_wait(barrier, 27)
+            pl.semaphore_wait(barrier, 14)
+            greet(0)
         for d in range(8):
             @pl.when(d != me)
             def _():
-                copy_a(p, d, me, core, my_rows).start()
+                copy_a(p, d).start()
 
             @pl.when(d == me)
             def _():
                 recv_a[p, core, my_rows] = send_a[p, d]
 
     first = jnp.logical_and(x == 0, z == 0)
-    loads[3].wait()
-
-    def copy_u(k, source):
-        return pltpu.make_async_remote_copy(
-            src_ref=send_u.at[k], dst_ref=recv_u.at[pl.ds(pl.multiple_of(64 * source, 64), 64)],
-            send_sem=su.at[k], recv_sem=ru.at[source], device_id={Y: k},
+    loads[2].wait()
+
+    def copy_u(k):
+        return pltpu.make_async_remote_copy(
+            src_ref=send_u.at[k], dst_ref=recv_u.at[my_rows],
+            send_sem=su, recv_sem=ru, device_id={Y: k},
         )
 
     @pl.when(first)
@@ -199,13 +212,13 @@
         for k in range(4):
             @pl.when(k != y)
             def _():
-                copy_u(k, y).start()
+                copy_u(k).start()
 
             @pl.when(k == y)
             def _():
                 recv_u[my_rows] = send_u[k]
 
-    for i in (2, 4, 5, 6, 7):
+    for i in (1, 3, 4, 5, 6):
         loads[i].wait()
     gain = 1.0 / (1.0 + STEP * (mrow[...] + mcol[0:1, :]))
     w = Weights(STEP * (mpack[...] + mcol[0:1, :]))
@@ -218,12 +231,12 @@
         t, c = powers[-1]
         powers.append((hop * t, hop * c + cross * t))
 
+    pl.semaphore_wait(met.at[0], 2)
+    greet(1)
+
     @pl.when(first)
     def _():
-        for k in range(4):
-            @pl.when(k != y)
-            def _():
-                copy_u(k, k).wait_recv()
+        taken(ru, send_u.at[pl.ds(0, 3)])
         modes = dot(table, recv_u[...])
         group = lane_group()
         total = jnp.where(group == 0, modes[0:64], 0.0)
@@ -236,10 +249,10 @@
         start_c[...] = jnp.zeros_like(start_c)
 
     for p in range(PHASES):
-        for s in range(8):
-            @pl.when(s != me)
-            def _():
-                copy_a(p, s, s, s % 2, pl.ds(64 * (s // 2), 64)).wait_recv()
+        taken(ra.at[p], send_a.at[p, pl.ds(0, 7)])
+        if p == 0:
+            pl.semaphore_wait(met.at[1], 2)
+            greet(2)
         for h in range(2):
             src[p, h] = gain * dot(table, recv_a[p, h])
 
@@ -261,15 +274,16 @@
         send_z[2 * v] = jnp.where(lower, a, pltpu.roll(b, 4, 0))
         send_z[2 * v + 1] = jnp.where(lower, pltpu.roll(a, 4, 0), b)
 
-    def copy_z(to, source):
-        return pltpu.make_async_remote_copy(
-            src_ref=send_z.at[to], dst_ref=recv_z.at[source],
-            send_sem=sz.at[to], recv_sem=rz.at[source], device_id={Z: to},
-        )
-
+    def copy_z(to):
+        return pltpu.make_async_remote_copy(
+            src_ref=send_z.at[to], dst_ref=recv_z.at[z],
+            send_sem=sz, recv_sem=rz, device_id={Z: to},
+        )
+
+    pl.semaphore_wait(met.at[2], 2)
     far_first = sorted(range(1, NZ), key=lambda k: -min(k, NZ - k))
     for k in far_first:
-        copy_z(lax.rem(z + k, NZ), z).start()
+        copy_z(lax.rem(z + k, NZ)).start()
     recv_z[z] = send_z[z]
 
     send_n[0] = points[1][3]
@@ -280,9 +294,7 @@
     )
     copy_n.start()
 
-    for k in far_first[::-1]:
-        source = lax.rem(z + k, NZ)
-        copy_z(source, source).wait_recv()
+    taken(rz, send_z.at[pl.ds(0, NZ - 1)])
     plain, coupled = [jnp.zeros((8, 128), F32)], [jnp.zeros((8, 128), F32)]
     for k in range(NZ):
         plain.append(hop * plain[-1] + recv_z[k])
@@ -291,16 +303,14 @@
     states = [a + b for a, b in zip(plain, coupled)]
     send_x[...] = states[NZ]
 
-    def copy_x(to, source, k):
-        return pltpu.make_async_remote_copy(
-            src_ref=send_x, dst_ref=recv_x.at[source], send_sem=sx.at[k], recv_sem=rx.at[source], device_id={X: to}
+    def copy_x(to):
+        return pltpu.make_async_remote_copy(
+            src_ref=send_x, dst_ref=recv_x.at[x], send_sem=sx, recv_sem=rx, device_id={X: to}
         )
 
     for k in range(1, NX):
-        copy_x(lax.rem(x + k, NX), x, k).start()
-    for k in range(1, NX):
-        source = lax.rem(x + k, NX)
-        copy_x(source, source, k).wait_recv()
+        copy_x(lax.rem(x + k, NX)).start()
+    taken(rx, recv_x.at[pl.ds(0, NX - 1)])
     recv_x[x] = states[NZ]
     entering = jnp.zeros((8, 128), F32)
     for k in range(NX - 1):
@@ -310,14 +320,14 @@
     for k in range(NZ):
         send_b[k] = states[k] + (powers[k][0] * entering + powers[k][1] * turned)
 
-    def copy_b(to, source):
-        return pltpu.make_async_remote_copy(
-            src_ref=send_b.at[to], dst_ref=recv_b.at[source],
-            send_sem=sb.at[to], recv_sem=rb.at[source], device_id={Z: to},
+    def copy_b(to):
+        return pltpu.make_async_remote_copy(
+            src_ref=send_b.at[to], dst_ref=recv_b.at[z],
+            send_sem=sb, recv_sem=rb, device_id={Z: to},
         )
 
     for k in far_first:
-        copy_b(lax.rem(z + k, NZ), z).start()
+        copy_b(lax.rem(z + k, NZ)).start()
     recv_b[z] = send_b[z]
 
     copy_n.wait_recv()
@@ -327,9 +337,7 @@
     near_d = [near[1], weighted(w.w4, points[0]) + w.d2 * near[0]]
     near_e = [near[2], weighted(w.w3, points[0]) + w.e2 * near[0]]
 
-    for k in far_first[::-1]:
-        source = lax.rem(z + k, NZ)
-        copy_b(source, source).wait_recv()
+    taken(rb, send_b.at[pl.ds(0, NZ - 1)])
     fs, gs = [], []
     for v in range(8):
         a, b = recv_b[2 * v], recv_b[2 * v + 1]
@@ -358,8 +366,7 @@
         enter = a + e1 + d + e2
         if h == 0:
             enter = enter + start
-        squares = [jnp.sum(q * q, axis=0, keepdims=True) for q in r1 + r2 + p1 + p2 + v1 + v2]
-        sums.append(squares)
+        sums.append(r1 + r2 + p1 + p2 + v1 + v2)
         begin = jnp.concatenate(turn([enter, v2[0], v2[1], v2[2]]), axis=0)
         ends = jnp.concatenate(turn(v2), axis=0)
         u = begin
@@ -368,10 +375,15 @@
             src[p, h] = u
         src[3, h] = ends
 
-    def copy_o(p, h, k, source):
-        return pltpu.make_async_remote_copy(
-            src_ref=send_o.at[p, h, pl.ds(64 * k, 64)], dst_ref=recv_o.at[p, source],
-            send_sem=so.at[p, h, k], recv_sem=ro.at[p, source], device_id={Y: k, CORE: h},
+    def copy_o(p, h, k):
+        return pltpu.make_async_remote_copy(
+            src_ref=send_o.at[p, h, pl.ds(64 * k, 64)], dst_ref=recv_o.at[p, me],
+            send_sem=so, recv_sem=ro.at[p], device_id={Y: k, CORE: h},
+        )
+
+    def copy_s(h, k):
+        return pltpu.make_async_remote_copy(
+            src_ref=send_s.at[h], dst_ref=recv_s.at[me], send_sem=ss, recv_sem=rs, device_id={Y: k, CORE: h}
         )
 
     rest = sr[...]
@@ -385,91 +397,65 @@
             for k in range(4):
                 @pl.when(2 * k + h != me)
                 def _():
-                    copy_o(p, h, k, me).start()
+                    copy_o(p, h, k).start()
 
                 @pl.when(2 * k + h == me)
                 def _():
                     recv_o[p, me] = send_o[p, h, 64 * k : 64 * k + 64]
-
-    def copy_s(h, k, source):
-        return pltpu.make_async_remote_copy(
-            src_ref=send_s.at[h], dst_ref=recv_s.at[source],
-            send_sem=ss.at[h, k], recv_sem=rs.at[source], device_id={Y: k, CORE: h},
-        )
-
-    for h in range(2):
-        send_s[h] = jnp.concatenate(sums[h], axis=0)
-    for h in range(2):
-        for k in range(4):
-            @pl.when(2 * k + h != me)
-            def _():
-                copy_s(h, k, me).start()
-
-            @pl.when(2 * k + h == me)
-            def _():
-                recv_s[me] = send_s[h]
-
-    stores = []
+        if p == 1:
+            for h in range(2):
+                send_s[h] = jnp.concatenate([jnp.sum(q * q, axis=0, keepdims=True) for q in sums[h]], axis=0)
+            for h in range(2):
+                for k in range(4):
+                    @pl.when(2 * k + h != me)
+                    def _():
+                        copy_s(h, k).start()
+
+                    @pl.when(2 * k + h == me)
+                    def _():
+                        recv_s[me] = send_s[h]
     for p in range(PHASES):
-        for s in range(8):
-            @pl.when(s != me)
-            def _():
-                copy_o(p, s % 2, s // 2, s).wait_recv()
-        sides = []
-        for side in range(2):
-            sides.append(turn([recv_o[p, 4 * side + q].astype(F32) for q in range(4)]))
-        rows = jnp.concatenate(
+        if p == 3:
+            taken(rs, recv_s.at[pl.ds(0, 7)])
+            total = recv_s[0]
+            for s in range(1, 8):
+                total = total + recv_s[s]
+            total = jnp.sum(total, axis=1, keepdims=True)
+            norms = jnp.sqrt(total[0:8] / (GRID * GRID))
+            ratios = jnp.sqrt(total[8:16] / total[16:24])
+            mine = lax.broadcasted_iota(jnp.int32, (8, 128), 1) == lax.broadcasted_iota(jnp.int32, (8, 128), 0) % 4
+            for column, result in ((norms, history), (ratios, change)):
+                spread = jnp.where(mine, column, 0.0)
+                for i in range(2):
+                    result[i : i + 1, :] = jnp.sum(spread[4 * i : 4 * i + 4], axis=0, keepdims=True)[:, 0:4]
+        taken(ro.at[p], send_a.at[p, pl.ds(0, 7)])
+        sides = [turn([recv_o[p, 4 * side + q].astype(F32) for q in range(4)]) for side in range(2)]
+        stacked = jnp.concatenate(
             [jnp.concatenate([sides[0][c], sides[1][c]], axis=1) for c in range(4)], axis=0
         ).astype(BF16)
-        field = dot(rows, table)
+        field = dot(stacked, table)
         for c in range(4):
             hout[4 * c + p] = field[64 * c : 64 * c + 64]
-            stores.append(pltpu.make_async_copy(hout.at[4 * c + p], heat.at[4 * c + p], store_sem.at[4 * c + p]))
-            stores[-1].start()
-
-    for s in range(8):
-        @pl.when(s != me)
-        def _():
-            copy_s(s % 2, s // 2, s).wait_recv()
-    total = recv_s[0]
-    for s in range(1, 8):
-        total = total + recv_s[s]
-    total = jnp.sum(total, axis=1, keepdims=True)
-    norms = jnp.sqrt(total[0:8] / (GRID * GRID))
-    ratios = jnp.sqrt(total[8:16] / total[16:24])
-    mine = lax.broadcasted_iota(jnp.int32, (8, 128), 1) == lax.broadcasted_iota(jnp.int32, (8, 128), 0) % 4
-    for column, out in ((norms, history), (ratios, change)):
-        spread = jnp.where(mine, column, 0.0)
-        for i in range(2):
-            out[i : i + 1, :] = jnp.sum(spread[4 * i : 4 * i + 4], axis=0, keepdims=True)[:, 0:4]
-
-    for p in range(PHASES):
-        for d in range(8):
-            @pl.when(d != me)
-            def _():
-                copy_a(p, d, me, core, my_rows).wait_send()
-                copy_o(p, d % 2, d // 2, me).wait_send()
-
-    for d in range(8):
-        @pl.when(d != me)
-        def _():
-            copy_s(d % 2, d // 2, me).wait_send()
+
+    taken(sa, send_a.at[:, pl.ds(0, 7)])
+    taken(so, send_a.at[:, pl.ds(0, 7)])
+    taken(ss, recv_s.at[pl.ds(0, 7)])
 
     @pl.when(first)
     def _():
-        for k in range(4):
-            @pl.when(k != y)
-            def _():
-                copy_u(k, y).wait_send()
+        taken(su, send_u.at[pl.ds(0, 3)])
 
     copy_n.wait_send()
-    for k in range(1, NZ):
-        to = lax.rem(z + k, NZ)
-        copy_z(to, z).wait_send()
-        copy_b(to, z).wait_send()
-    for k in range(1, NX):
-        copy_x(lax.rem(x + k, NX), x, k).wait_send()
-    for copy in stores:
+    taken(sz, send_z.at[pl.ds(0, NZ - 1)])
+    taken(sb, send_b.at[pl.ds(0, NZ - 1)])
+    taken(sx, recv_x.at[pl.ds(0, NX - 1)])
+
+
+def put_out(a, b, c, heat, history, change, sem):
+    copies = [pltpu.make_async_copy(s, d, sem.at[i]) for i, (s, d) in enumerate(((a, heat), (b, history), (c, change)))]
+    for copy in copies:
+        copy.start()
+    for copy in copies:
         copy.wait()
 
 
@@ -480,7 +466,7 @@
     vmem = pl.BlockSpec(memory_space=pltpu.VMEM)
     dma = pltpu.SemaphoreType.DMA
     scratch = [
-        pltpu.VMEM((16, 64, 256), BF16), pltpu.VMEM((64, 256), BF16),
+        pltpu.VMEM((4, 4, 64, 256), BF16), pltpu.VMEM((64, 256), BF16),
         pltpu.VMEM((256, 256), BF16), pltpu.VMEM((256, 256), BF16),
         pltpu.VMEM((256, 128), F32), pltpu.VMEM((64, 128), F32),
         pltpu.VMEM((8, 128), F32), pltpu.VMEM((8, 128), F32),
@@ -492,23 +478,26 @@
         pltpu.VMEM((16, 8, 128), F32), pltpu.VMEM((16, 8, 128), F32),
         pltpu.VMEM((4, 2, 256, 128), BF16), pltpu.VMEM((4, 8, 64, 128), BF16),
         pltpu.VMEM((2, 24, 128), F32), pltpu.VMEM((8, 24, 128), F32),
-        pltpu.VMEM((16, 64, 256), F32),
-        dma((8,)), dma((16,)), dma((4, 8)), dma((4, 8)), dma((4,)), dma((4,)), dma, dma,
-        dma((16,)), dma((16,)), dma((4,)), dma((4,)), dma((16,)), dma((16,)),
-        dma((4, 2, 4)), dma((4, 8)), dma((2, 4)), dma((8,)),
+        dma((11,)), pltpu.SemaphoreType.REGULAR((3,)), dma, dma((4,)), dma, dma, dma, dma,
+        dma, dma, dma, dma, dma, dma, dma, dma((4,)), dma, dma,
     ]
-    return pl.pallas_call(
+    shapes = (forcing.shape, (2, 4), (2, 4))
+    results = pl.pallas_call(
         kernel,
-        out_shape=(
-            jax.ShapeDtypeStruct((16, 64, 256), F32),
-            jax.ShapeDtypeStruct((2, 4), F32),
-            jax.ShapeDtypeStruct((2, 4), F32),
-        ),
+        out_shape=tuple(pltpu.VMEM(shape, F32) for shape in shapes),
         in_specs=[anywhere] * 8,
-        out_specs=(anywhere, vmem, vmem),
+        out_specs=(vmem,) * 3,
         scratch_shapes=scratch,
         compiler_params=pltpu.CompilerParams(collective_id=0, has_side_effects=True),
     )(forcing, starting_heat, half, rest, *tables)
+    results = [pltpu.with_memory_space_constraint(a, pltpu.VMEM) for a in results]
+    return pl.pallas_call(
+        put_out,
+        out_shape=tuple(jax.ShapeDtypeStruct(shape, F32) for shape in shapes),
+        in_specs=[vmem] * 3,
+        out_specs=(anywhere,) * 3,
+        scratch_shapes=[dma((3,))],
+    )(*results)
 
 
 def solution(mesh):

time: 59.3 us -> 49.5 us (0.83)
  Pallas kernels: 54.9 us -> 48.7 us
  local copies, waits for them, and re-layouts: 3.52 us -> 0 us
    pallas_call x1 -> x2, Pallas kernels: 54.9 us -> 48.7 us  [the longest x1 47.7 us: per_device(): pl.pallas_call(kernel, out_shape=tuple((pltpu.VMEM(shape, F32) for shape...]
    unnamed x7 -> x0, local copies, waits for them, and re-layouts: 3.52 us -> none
where the time goes in v3:
time: 49.5 us; the launch traced here: 49.3 us
  Pallas kernels  48.7 us (98%)
  between operations  0.64 us (1%)
    pallas_call x1, Pallas kernels, per_device(): pl.pallas_call(kernel, out_shape=tuple((pltpu.VMEM(shape, F32) for shape...  47.7 us
    pallas_call x1, Pallas kernels, per_device(): pl.pallas_call(put_out, out_shape=tuple((jax.ShapeDtypeStruct(shape, F32)...  1 us

profile of v3, /device:TPU:1, one launch (start us, length us, event | category | flops | bytes accessed | tf_op | source)
XLA Modules:
  0.0 49.3 jit_solution(1749241053559962790)
XLA Ops:
  0.6 47.7 %shard_map.103 = (f32[16,64,256]{2,1,0:T(8,128)S(1)}, f32[2,4]{1,0:T(2,128)S(1)}, f32[2,4]{1,0:T(2,128)S(1)}) custom-call(bf16[16,64,256]{2,1,0:T(8,128)(2,1)} %forcing.1, bf16[64,256]{1,0:T(8,128)(2,1)} %starting.1, bf16[256,256]{1,0:T(8,128)(2,1)} %constant.12.clone.sine, bf16[256,256]{1,0:T(8,128)(2,1)} %constant.13.clone.sine_rest, ...), custom_call_target="tpu_custom_call" | custom-call | tf_op jit(solution)/shard_map/pallas_call | solution.py:485
  48.3 1.0 %shard_map.104 = (f32[16,64,256]{2,1,0:T(8,128)}, f32[2,4]{1,0:T(2,128)}, f32[2,4]{1,0:T(2,128)}) custom-call(f32[16,64,256]{2,1,0:T(8,128)S(1)} %get-tuple-element.6.a, f32[2,4]{1,0:T(2,128)S(1)} %get-tuple-element.7.b, f32[2,4]{1,0:T(2,128)S(1)} %get-tuple-element.8.c), custom_call_target="tpu_custom_call" | custom-call | tf_op jit(solution)/shard_map/pallas_call | solution.py:494
